TPU v7x, 256 devices: a whole 4x4x8 slice. The times are simulated.
256 devices in a mesh: tp: 4 (over x), rep: 64 (over y, z, core).
Axes of the slice: x: 4, y: 4, z: 8, core: 2. Of those that a mesh axis runs over, the one named last changes fastest.
Arguments:
- queries: bfloat16 [1024, 4096], P('rep', 'tp'), may hold values from -6 to 6
- new_keys: bfloat16 [1024, 2048], P('rep', 'tp'), may hold values from -6 to 6
- new_values: bfloat16 [1024, 2048], P('rep', 'tp'), may hold values from -6 to 6
- stored_keys: bfloat16 [1024, 16, 128, 128], P('rep', 'tp'), may hold values from -6 to 6
- stored_values: bfloat16 [1024, 16, 128, 128], P('rep', 'tp'), may hold values from -6 to 6
- lengths: int32 [1024], P('rep'), may hold values from 1 to 128
- out_proj: bfloat16 [4096, 4608], P('tp', 'rep'), may hold values from -0.09375 to 0.09375
- residual: bfloat16 [1024, 4608], P(None, 'rep'), may hold values from -4.5 to 4.5
- norm_gain: float32 [4608], replicated, may hold values from 0.1 to 1.9
- embedding: bfloat16 [256000, 4608], P(('tp', 'rep')), may hold values from -1.25 to 1.25
- targets: int32 [1024], replicated, may hold values from 0 to 255999
- old_sums: float32 [1024], P('rep'), may hold values from -3 to 0
- rewards: float32 [1024], P('rep'), may hold values from -6 to 6
- group_ids: int32 [1024], P('rep'), may hold values from 0 to 127, as said below
Outputs:
- logprob_sum: float32 [1024], P('rep')
- advantage: float32 [1024], P('rep')
Inputs may be any that keep to these rules, and one draw needn't show every extreme that they name: `group_ids`: each id names exactly 8 continuations.
All inputs are finite; a program needn't handle non-finite values.
Results may differ from a plain program's by a relative error of at most 0.001.
Values may be sent and summed in bfloat16 or wider, within the bound.
No kernel may reach another device: no remote copies, remote signals or barrier semaphores. Data moves between devices by JAX's collectives and lax.ppermute only.
A program may use at most 64 MiB of HBM per device.

v0:
```python
import jax
import jax.numpy as jnp
from jax import lax
from jax.sharding import Mesh
from jax.sharding import PartitionSpec as P

D = 4608
GROUP = 8
REP = ("rep_0", "rep_1", "rep_2")
TP_REP = ("tp", "rep_0", "rep_1", "rep_2")


def sent_to_all(x, axis):
    devices = lax.axis_size(axis)
    return lax.all_to_all(jnp.broadcast_to(x[None], (devices, *x.shape)), axis, 0, 0, tiled=True)


def of_everyone(x, axis):
    everything = sent_to_all(x, axis)
    return jnp.sum(everything, axis=0)


def laid_out(blocks, dim):
    lengths = list(blocks.shape[1:])
    lengths[dim] *= blocks.shape[0]
    return jnp.moveaxis(blocks, 0, dim).reshape(lengths)


def whole_of(x, axes, dim):
    far, near = axes
    blocks = sent_to_all(sent_to_all(x, far), near)
    return laid_out(blocks.swapaxes(0, 1).reshape(-1, *x.shape), dim)


def over_axes(x, axes):
    far, near = axes
    nearer = of_everyone(x, near)
    return of_everyone(nearer, far)


def packed_total(arrays, axis):
    ravelled, at, finished = (jnp.concatenate([a.reshape(-1) for a in arrays]), 0, [])
    subtotal = over_axes(ravelled, axis)
    for a in arrays:
        finished.append(subtotal[at : at + a.size].reshape(a.shape))
        at += a.size
    return tuple(finished)


def attention(queries, new_keys, new_values, stored_keys, stored_values, lengths):
    samp, heads_kv, span, depth = stored_keys.shape
    sample_ratio = queries.shape[1] // (heads_kv * depth)
    query_vector = queries.reshape(samp, heads_kv, sample_ratio, depth)
    scores = (
        jnp.einsum("sgqd,sgpd->sgqp", query_vector, stored_keys, preferred_element_type=jnp.float32)
        / 12.0
    )
    scores = 50.0 * jnp.tanh(scores / 50.0)
    valid = lax.broadcasted_iota(jnp.int32, (samp, 1, 1, span), 3) < lengths[:, None, None, None]
    expo = jnp.where(valid, jnp.exp(scores), 0.0)
    own_logit = (
        jnp.einsum(
            "sgqd,sgd->sgq",
            query_vector,
            new_keys.reshape(samp, heads_kv, depth),
            preferred_element_type=jnp.float32,
        )
        / 12.0
    )
    own_logit = 50.0 * jnp.tanh(own_logit / 50.0)
    own_exp = jnp.exp(own_logit)
    total = jnp.sum(expo, -1) + own_exp
    probs = (expo / total[..., None]).astype(jnp.bfloat16)
    own_probability = (own_exp / total).astype(jnp.bfloat16)
    attended_output = jnp.einsum(
        "sgqp,sgpd->sgqd", probs, stored_values, preferred_element_type=jnp.float32
    )
    attended_output = attended_output + own_probability.astype(jnp.float32)[
        ..., None
    ] * new_values.reshape(samp, heads_kv, 1, depth).astype(jnp.float32)
    return attended_output.reshape(samp, sample_ratio * heads_kv * depth).astype(jnp.bfloat16)


def per_device(
    queries,
    new_keys,
    new_values,
    stored_keys,
    stored_values,
    lengths,
    out_proj,
    residual,
    norm_gain,
    embedding,
    targets,
    old_sums,
    rewards,
    group_ids,
):
    samp = queries.shape[0]
    reps = lax.axis_size(REP)
    rep_index = lax.axis_index(REP)
    tp_index = lax.axis_index("tp")
    groups = samp * reps // GROUP
    member = group_ids[:, None] == lax.broadcasted_iota(jnp.int32, (1, groups), 1)
    reward_part = jnp.sum(jnp.where(member, rewards[:, None], 0.0), 0)
    group_total = of_everyone(reward_part, REP)
    mine = jnp.sum(jnp.where(member, group_total[None, :], 0.0), 1)
    advantage = rewards - (mine - rewards) / (GROUP - 1.0)
    context = attention(queries, new_keys, new_values, stored_keys, stored_values, lengths)
    partial_value = jnp.dot(
        whole_of(context, (("rep_0", "rep_1"), "rep_2"), 0),
        out_proj,
        preferred_element_type=jnp.float32,
    )
    columns = residual.shape[1]
    vocab_rows = embedding.shape[0]
    contract = (((1,), (1,)), ((), ()))
    heads = of_everyone(partial_value, "tp")
    stream = residual.astype(jnp.float32) + heads
    squares = of_everyone(jnp.sum(stream * stream, 1), REP)
    scale = lax.rsqrt(squares / D + 1e-06)
    gain_part = lax.dynamic_slice_in_dim(norm_gain, rep_index * columns, columns)
    normed = (stream * scale[:, None] * gain_part[None, :]).astype(jnp.bfloat16)
    gathered = lax.all_gather(normed, REP, axis=1, tiled=True)
    logits = lax.dot_general(gathered, embedding, contract, preferred_element_type=jnp.float32)
    capped = 30.0 * jnp.tanh(logits / 30.0)
    offset = (tp_index * reps + rep_index) * vocab_rows
    entry_ids = offset + lax.broadcasted_iota(jnp.int32, (1, vocab_rows), 1)
    picked_part = jnp.sum(jnp.where(entry_ids == targets[:, None], capped, 0.0), 1)
    total, picked = packed_total(
        (jnp.sum(jnp.exp(capped), 1), picked_part), (("tp", "rep_0"), ("rep_1", "rep_2"))
    )
    logprob = picked - jnp.log(total)
    own_rows = lax.dynamic_slice_in_dim(logprob, rep_index * samp, samp)
    logprob_sum = old_sums + own_rows
    return (logprob_sum, advantage)


def solution(mesh):
    split = Mesh(mesh.devices.reshape(mesh.shape["tp"], 4, 8, 2), ("tp", "rep_0", "rep_1", "rep_2"))
    placed = (
        P(REP, "tp"),
        P(REP, "tp"),
        P(REP, "tp"),
        P(REP, "tp", None, None),
        P(REP, "tp", None, None),
        P(REP),
        P("tp", REP),
        P(None, REP),
        P(),
        P(TP_REP, None),
        P(),
        P(REP),
        P(REP),
        P(REP),
    )
    return jax.shard_map(
        per_device, mesh=split, in_specs=placed, out_specs=(P(REP), P(REP)), check_vma=False
    )
```

profile of v0, /device:TPU:1, one launch (start us, length us, event | category | flops | bytes accessed | tf_op | source)
XLA Modules:
  0.0 235.7 jit_solution(11303239664290411377)
XLA Ops:
  7.2 0.9 reshape.88
  8.1 0.7 iota_compare_fusion.1
  8.8 1.3 fusion.12
  10.2 0.7 reshape.94
  11.0 0.2 fusion.13
  11.5 0.7 reshape.90
  12.3 2.3 fusion.4
  14.7 36.7 %all_to_all.39 = bf16[32,16,1024]{2,1,0:T(8,128)(2,1)S(1)} all-to-all(bf16[32,16,1024]{2,1,0:T(8,128)(2,1)S(1)} %broadcast_in_dim.53), channel_id=1, replica_groups=mesh['tp'=4,'rep_0'=4,'rep_1'=8,'rep_2'=2] {'rep_0','rep_1'}, dimensions={0} | all-to-all | bytes 2097152 | tf_op jit(solution)/shard_map/all_to_all | solution.py:15
  51.4 0.3 broadcast_in_dim.55
  51.7 9.9 %all_to_all.40 = bf16[2,32,16,1024]{3,2,1,0:T(8,128)(2,1)S(1)} all-to-all(bf16[2,32,16,1024]{3,2,1,0:T(8,128)(2,1)S(1)} %broadcast_in_dim.55), channel_id=1, replica_groups=mesh['tp'=4,'rep_0'=4,'rep_1'=8,'rep_2'=2] {'rep_2'}, dimensions={0} | all-to-all | bytes 4194304 | tf_op jit(solution)/shard_map/all_to_all | solution.py:15
  61.6 0.3 copy.35
  61.9 0.8 fusion.14
  62.9 19.5 %all_to_all.41 = f32[4,1024,72]{1,2,0:T(8,128)S(1)} all-to-all(f32[4,1024,72]{1,2,0:T(8,128)S(1)} %broadcast_in_dim.56), channel_id=1, replica_groups=mesh['tp'=4,'rep_0'=4,'rep_1'=8,'rep_2'=2] {'tp'}, dimensions={0} | all-to-all | bytes 2359296 | tf_op jit(solution)/shard_map/all_to_all | solution.py:15
  82.3 0.8 reduce_sum.100
  83.1 1.0 multiply_reduce_fusion
  84.2 0.8 broadcast_in_dim.57
  85.0 7.1 %all-to-all-start.3 = ((f32[64,1,1024]{2,1,0:T(1,128)}), f32[64,1,1024]{2,1,0:T(1,128)S(1)}, u32[]{:S(2)}, u32[]{:S(2)}) async-start(f32[64,1,1024]{2,1,0:T(1,128)} %broadcast_in_dim.57), calls=%async_computation.3 | async-start | bytes 524288 | tf_op jit(solution)/shard_map/all_to_all | solution.py:15
  92.1 0.8 dynamic_slice.6
  92.9 11.1 %all-to-all-done.3 = f32[64,1,1024]{2,1,0:T(1,128)S(1)} async-done(((f32[64,1,1024]{2,1,0:T(1,128)}), f32[64,1,1024]{2,1,0:T(1,128)S(1)}, u32[]{:S(2)}, u32[]{:S(2)}) %all-to-all-start.3) | async-done | bytes 262176 | tf_op jit(solution)/shard_map/all_to_all | solution.py:15
  104.2 1.7 multiply_convert_fusion
  106.1 0.6 broadcast_in_dim.100
  106.7 6.0 %all-to-all-start.6 = ((f32[64,1,128]{2,1,0:T(1,128)}), f32[64,1,128]{2,1,0:T(1,128)S(1)}, u32[]{:S(2)}, u32[]{:S(2)}) async-start(f32[64,1,128]{2,1,0:T(1,128)} %broadcast_in_dim.100), calls=%async_computation.6 | async-start | bytes 65536 | tf_op jit(solution)/shard_map/all_to_all | solution.py:15
  112.8 72.8 %all-gather.2.cloned.1.call-done = bf16[1024,4608]{0,1:T(8,128)(2,1)} async-done(((bf16[1024,72]{0,1:T(8,128)(2,1)}), bf16[1024,4608]{0,1:T(8,128)(2,1)}) %all-gather.2.cloned.1.call-update) | async-done | bytes 9437200 | tf_op jit(solution)/shard_map/all_gather | solution.py:125
  185.6 15.7 %exponential_reduce_fusion = (f32[1024]{0:T(1024)S(1)}, f32[1024]{0:T(1024)S(1)}) fusion(s32[1024]{0:T(1024)S(1)} %copy-done.4, s32[1000]{0:T(1024)S(1)} %iota_add_fusion, bf16[1024,4608]{0,1:T(8,128)(2,1)} %all-gather.2.cloned.1.call-done, bf16[1000,4608]{1,0:T(8,128)(2,1)} %param.23), kind=kOutput, calls=%fused_computation.1 | convolution fusion | flops 9443325952 | bytes 18669472 | tf_op jit(solution)/shard_map/dot_general | solution.py:126
  201.4 0.7 broadcast_in_dim.59
  202.1 4.7 %all-to-all-start.4 = ((f32[16,1,2048]{2,1,0:T(1,128)}), f32[16,1,2048]{2,1,0:T(1,128)S(1)}, u32[]{:S(2)}, u32[]{:S(2)}) async-start(f32[16,1,2048]{2,1,0:T(1,128)} %broadcast_in_dim.59), calls=%async_computation.4 | async-start | bytes 262144 | tf_op jit(solution)/shard_map/all_to_all | solution.py:15
  206.9 8.7 %all-to-all-done.4 = f32[16,1,2048]{2,1,0:T(1,128)S(1)} async-done(((f32[16,1,2048]{2,1,0:T(1,128)}), f32[16,1,2048]{2,1,0:T(1,128)S(1)}, u32[]{:S(2)}, u32[]{:S(2)}) %all-to-all-start.4) | async-done | bytes 131104 | tf_op jit(solution)/shard_map/all_to_all | solution.py:15
  215.7 0.7 broadcast_in_dim.60
  216.4 5.0 %all-to-all-start.5 = ((f32[16,1,2048]{2,1,0:T(1,128)}), f32[16,1,2048]{2,1,0:T(1,128)S(1)}, u32[]{:S(2)}, u32[]{:S(2)}) async-start(f32[16,1,2048]{2,1,0:T(1,128)} %broadcast_in_dim.60), calls=%async_computation.5 | async-start | bytes 262144 | tf_op jit(solution)/shard_map/all_to_all | solution.py:15
  221.4 0.5 multiply_subtract_fusion
  221.9 6.3 %all-to-all-done.5 = f32[16,1,2048]{2,1,0:T(1,128)S(1)} async-done(((f32[16,1,2048]{2,1,0:T(1,128)}), f32[16,1,2048]{2,1,0:T(1,128)S(1)}, u32[]{:S(2)}, u32[]{:S(2)}) %all-to-all-start.5) | async-done | bytes 131104 | tf_op jit(solution)/shard_map/all_to_all | solution.py:15
  228.3 0.6 dynamic-slice_add_fusion
  (35 shorter events, 1.5 us)
Async XLA Ops:
  7.2 1.7 copy-start
  51.7 10.2 %copy-start.2 = (bf16[1024,72]{0,1:T(8,128)(2,1)S(1)}, bf16[1024,72]{0,1:T(8,128)(2,1)}, u32[]{:S(2)}) copy-start(bf16[1024,72]{0,1:T(8,128)(2,1)} %param.20) | copy-start | bytes 442372
  61.9 21.2 %copy-start.1 = (bf16[1024,72]{0,1:T(8,128)(2,1)S(1)}, bf16[1024,72]{0,1:T(8,128)(2,1)}, u32[]{:S(2)}) copy-start(bf16[1024,72]{0,1:T(8,128)(2,1)} %param.21) | copy-start | bytes 442372
  62.7 43.2 %copy-start.5 = (s32[16]{0:T(128)S(1)}, s32[16]{0:T(128)}, u32[]{:S(2)}) copy-start(s32[16]{0:T(128)} %param.27) | copy-start | bytes 196
  62.7 43.2 %copy-start.6 = (f32[16]{0:T(128)S(1)}, f32[16]{0:T(128)}, u32[]{:S(2)}) copy-start(f32[16]{0:T(128)} %param.26) | copy-start | bytes 196
  62.7 122.9 %copy-start.4 = (s32[1024]{0:T(1024)S(1)}, s32[1024]{0:T(1024)}, u32[]{:S(2)}) copy-start(s32[1024]{0:T(1024)} %param.24) | copy-start | bytes 12292
  85.0 19.0 %all-to-all-start.3 = ((f32[64,1,1024]{2,1,0:T(1,128)}), f32[64,1,1024]{2,1,0:T(1,128)S(1)}, u32[]{:S(2)}, u32[]{:S(2)}) async-start(f32[64,1,1024]{2,1,0:T(1,128)} %broadcast_in_dim.57), calls=%async_computation.3 | async-start | bytes 524288 | tf_op jit(solution)/shard_map/all_to_all | solution.py:15
  92.0 93.6 %all-gather.2.cloned.1.call-start = ((), (), s32[]{:S(2)}) async-start(), calls=%async_computation.7 | async-start | bytes 9584640 | tf_op jit(solution)/shard_map/all_gather | solution.py:125
  106.7 94.7 %all-to-all-start.6 = ((f32[64,1,128]{2,1,0:T(1,128)}), f32[64,1,128]{2,1,0:T(1,128)S(1)}, u32[]{:S(2)}, u32[]{:S(2)}) async-start(f32[64,1,128]{2,1,0:T(1,128)} %broadcast_in_dim.100), calls=%async_computation.6 | async-start | bytes 65536 | tf_op jit(solution)/shard_map/all_to_all | solution.py:15
  112.7 115.5 %copy-start.3 = (f32[16]{0:T(128)S(1)}, f32[16]{0:T(128)}, u32[]{:S(2)}) copy-start(f32[16]{0:T(128)} %param.25) | copy-start | bytes 196
  202.1 13.5 %all-to-all-start.4 = ((f32[16,1,2048]{2,1,0:T(1,128)}), f32[16,1,2048]{2,1,0:T(1,128)S(1)}, u32[]{:S(2)}, u32[]{:S(2)}) async-start(f32[16,1,2048]{2,1,0:T(1,128)} %broadcast_in_dim.59), calls=%async_computation.4 | async-start | bytes 262144 | tf_op jit(solution)/shard_map/all_to_all | solution.py:15
  216.4 11.7 %all-to-all-start.5 = ((f32[16,1,2048]{2,1,0:T(1,128)}), f32[16,1,2048]{2,1,0:T(1,128)S(1)}, u32[]{:S(2)}, u32[]{:S(2)}) async-start(f32[16,1,2048]{2,1,0:T(1,128)} %broadcast_in_dim.60), calls=%async_computation.5 | async-start | bytes 262144 | tf_op jit(solution)/shard_map/all_to_all | solution.py:15
Sparse Core Ops, SparseCore 0:
  106.1 79.4 all-gather.1
where the time goes:
time: 237 us; the launch traced here: 236 us
  waiting for transfers between devices  98.9 us (42%)
  blocking collectives  66 us (28%)
  starting transfers between devices  22.8 us (10%)
  matrix products  20.3 us (9%)
  between operations  14.3 us (6%)
  local copies, waits for them, and re-layouts  7.36 us (3%)
  other arithmetic  6.06 us (3%)
    all_gather x1, waiting for transfers between devices, per_device(): gathered = lax.all_gather(normed, REP, axis=1, tiled=True)  72.8 us
    all_to_all x3, blocking collectives, sent_to_all(): lax.all_to_all(jnp.broadcast_to(x[None], (devices, *x.shape)), axis, 0, 0...  66 us
    all_to_all x4, waiting for transfers between devices, sent_to_all(): lax.all_to_all(jnp.broadcast_to(x[None], (devices, *x.shape)), axis, 0, 0...  26.1 us
    all_to_all x4, starting transfers between devices, sent_to_all(): lax.all_to_all(jnp.broadcast_to(x[None], (devices, *x.shape)), axis, 0, 0...  22.7 us
    dot_general x1, matrix products, per_device(): lax.dot_general(gathered, embedding, contract, preferred_element_type=jnp...  15.7 us
  transfers between devices with their start and end apart: 5, of which 4 were waited for; matrix products, arithmetic and copies ran while one was open for 8% of the time, Pallas kernels for 0%

commit v1 on v0

--- a/solution.py
+++ b/solution.py
@@ -122,7 +122,9 @@
     scale = lax.rsqrt(squares / D + 1e-06)
     gain_part = lax.dynamic_slice_in_dim(norm_gain, rep_index * columns, columns)
     normed = (stream * scale[:, None] * gain_part[None, :]).astype(jnp.bfloat16)
-    gathered = lax.all_gather(normed, REP, axis=1, tiled=True)
+    gathered = jnp.concatenate(
+        lax.all_to_all(jnp.stack([normed] * lax.axis_size(REP)), REP, 0, 0), axis=1
+    )
     logits = lax.dot_general(gathered, embedding, contract, preferred_element_type=jnp.float32)
     capped = 30.0 * jnp.tanh(logits / 30.0)
     offset = (tp_index * reps + rep_index) * vocab_rows

time: 237 us -> 371 us (1.57)
  waiting for transfers between devices: 98.9 us -> 234 us
  between operations: 14.3 us -> 0.87 us
  starting transfers between devices: 22.8 us -> 31.3 us
  local copies, waits for them, and re-layouts: 7.36 us -> 12.2 us
    all_to_all x0 -> x1, waiting for transfers between devices: none -> 208 us  [per_device(): lax.all_to_all(jnp.stack([normed] * lax.axis_size(REP)), REP, 0, 0)]
    all_gather x1 -> x0, waiting for transfers between devices: 72.8 us -> none  [per_device(): gathered = lax.all_gather(normed, REP, axis=1, tiled=True)]
    all_to_all x0 -> x1, starting transfers between devices: none -> 6.33 us  [per_device(): lax.all_to_all(jnp.stack([normed] * lax.axis_size(REP)), REP, 0, 0)]
    another operation x0 -> x1, local copies, waits for them, and re-layouts: none -> 4.86 us  [per_device(): jnp.stack([normed] * lax.axis_size(REP))]
  transfers between devices with their start and end apart: 5 -> 5, of which waited for: 4 -> 4; matrix products, arithmetic and copies ran while one was open for 8% -> 5% of each run, Pallas kernels for 0% -> 0%
where the time goes in v1:
time: 371 us; the launch traced here: 370 us
  waiting for transfers between devices  234 us (63%)
  blocking collectives  66 us (18%)
  starting transfers between devices  31.3 us (8%)
  matrix products  20.3 us (5%)
  local copies, waits for them, and re-layouts  12.2 us (3%)
  other arithmetic  5.4 us (1%)
    all_to_all x1, waiting for transfers between devices, per_device(): lax.all_to_all(jnp.stack([normed] * lax.axis_size(REP)), REP, 0, 0)  208 us
    all_to_all x3, blocking collectives, sent_to_all(): lax.all_to_all(jnp.broadcast_to(x[None], (devices, *x.shape)), axis, 0, 0...  66 us
    all_to_all x4, waiting for transfers between devices, sent_to_all(): lax.all_to_all(jnp.broadcast_to(x[None], (devices, *x.shape)), axis, 0, 0...  26.1 us
    all_to_all x4, starting transfers between devices, sent_to_all(): lax.all_to_all(jnp.broadcast_to(x[None], (devices, *x.shape)), axis, 0, 0...  24.9 us
    dot_general x1, matrix products, per_device(): lax.dot_general(gathered, embedding, contract, preferred_element_type=jnp...  15.7 us
  transfers between devices with their start and end apart: 5, of which 4 were waited for; matrix products, arithmetic and copies ran while one was open for 5% of the time, Pallas kernels for 0%

profile of v1, /device:TPU:1, one launch (start us, length us, event | category | flops | bytes accessed | tf_op | source)
XLA Modules:
  0.0 370.3 jit_solution(1938913209168502390)
XLA Ops:
  0.6 0.9 reshape.96
  1.6 0.7 iota_compare_fusion.1
  2.3 1.3 fusion.12
  3.7 0.7 reshape.104
  5.0 0.7 reshape.100
  5.7 2.3 fusion.4
  8.2 36.7 %all_to_all.44 = bf16[32,16,1024]{2,1,0:T(8,128)(2,1)S(1)} all-to-all(bf16[32,16,1024]{2,1,0:T(8,128)(2,1)S(1)} %broadcast_in_dim.53), channel_id=1, replica_groups=mesh['tp'=4,'rep_0'=4,'rep_1'=8,'rep_2'=2] {'rep_0','rep_1'}, dimensions={0} | all-to-all | bytes 2097152 | tf_op jit(solution)/shard_map/all_to_all | solution.py:15
  45.2 9.9 %all_to_all.45 = bf16[2,32,16,1024]{3,2,1,0:T(8,128)(2,1)S(1)} all-to-all(bf16[2,32,16,1024]{3,2,1,0:T(8,128)(2,1)S(1)} %broadcast_in_dim.55), channel_id=1, replica_groups=mesh['tp'=4,'rep_0'=4,'rep_1'=8,'rep_2'=2] {'rep_2'}, dimensions={0} | all-to-all | bytes 4194304 | tf_op jit(solution)/shard_map/all_to_all | solution.py:15
  55.1 0.3 copy.36
  55.4 0.8 fusion.14
  56.3 19.5 %all_to_all.46 = f32[4,1024,72]{1,2,0:T(8,128)S(1)} all-to-all(f32[4,1024,72]{1,2,0:T(8,128)S(1)} %broadcast_in_dim.56), channel_id=1, replica_groups=mesh['tp'=4,'rep_0'=4,'rep_1'=8,'rep_2'=2] {'tp'}, dimensions={0} | all-to-all | bytes 2359296 | tf_op jit(solution)/shard_map/all_to_all | solution.py:15
  75.8 0.8 reduce_sum.100
  76.6 1.0 multiply_reduce_fusion
  77.6 0.8 broadcast_in_dim.57
  78.4 7.1 %all-to-all-start.3 = ((f32[64,1,1024]{2,1,0:T(1,128)}), f32[64,1,1024]{2,1,0:T(1,128)S(1)}, u32[]{:S(2)}, u32[]{:S(2)}) async-start(f32[64,1,1024]{2,1,0:T(1,128)} %broadcast_in_dim.57), calls=%async_computation.3 | async-start | bytes 524288 | tf_op jit(solution)/shard_map/all_to_all | solution.py:15
  85.5 0.8 dynamic_slice.6
  86.3 11.2 %all-to-all-done.3 = f32[64,1,1024]{2,1,0:T(1,128)S(1)} async-done(((f32[64,1,1024]{2,1,0:T(1,128)}), f32[64,1,1024]{2,1,0:T(1,128)S(1)}, u32[]{:S(2)}, u32[]{:S(2)}) %all-to-all-start.3) | async-done | bytes 262176 | tf_op jit(solution)/shard_map/all_to_all | solution.py:15
  97.6 1.1 multiply_convert_fusion
  98.7 4.9 %stack.2 = bf16[64,1024,72]{1,2,0:T(8,128)(2,1)} broadcast(bf16[1024,72]{0,1:T(8,128)(2,1)S(1)} %multiply_convert_fusion), dimensions={1,2} | broadcast | bytes 9584640 | tf_op jit(solution)/shard_map/stack | solution.py:126
  103.6 6.3 %all-to-all-start.4 = ((bf16[64,1024,72]{1,2,0:T(8,128)(2,1)}), bf16[64,1024,72]{1,2,0:T(8,128)(2,1)}, u32[]{:S(2)}, u32[]{:S(2)}) async-start(bf16[64,1024,72]{1,2,0:T(8,128)(2,1)} %stack.2), calls=%async_computation.4 | async-start | bytes 18874368 | tf_op jit(solution)/shard_map/all_to_all | solution.py:126
  110.0 208.1 %all-to-all-done.4 = bf16[64,1024,72]{1,2,0:T(8,128)(2,1)} async-done(((bf16[64,1024,72]{1,2,0:T(8,128)(2,1)}), bf16[64,1024,72]{1,2,0:T(8,128)(2,1)}, u32[]{:S(2)}, u32[]{:S(2)}) %all-to-all-start.4) | async-done | bytes 9437216 | tf_op jit(solution)/shard_map/all_to_all | solution.py:126
  318.1 0.6 broadcast_in_dim.100
  318.8 5.8 %all-to-all-start.7 = ((f32[64,1,128]{2,1,0:T(1,128)}), f32[64,1,128]{2,1,0:T(1,128)S(1)}, u32[]{:S(2)}, u32[]{:S(2)}) async-start(f32[64,1,128]{2,1,0:T(1,128)} %broadcast_in_dim.100), calls=%async_computation.7 | async-start | bytes 65536 | tf_op jit(solution)/shard_map/all_to_all | solution.py:15
  324.6 15.7 %exponential_reduce_fusion = (f32[1024]{0:T(1024)S(1)}, f32[1024]{0:T(1024)S(1)}) fusion(s32[1024]{0:T(1024)S(1)} %copy-done.4, s32[1000]{0:T(1024)S(1)} %iota_add_fusion, bf16[1024,4608]{0,1:T(8,128)(2,1)} %bitcast.4, bf16[1000,4608]{1,0:T(8,128)(2,1)} %param.23), kind=kOutput, calls=%fused_computation.1 | convolution fusion | flops 9443325952 | bytes 18669472 | tf_op jit(solution)/shard_map/dot_general | solution.py:128
  340.4 0.7 broadcast_in_dim.59
  341.1 7.2 %all-to-all-start.5 = ((f32[16,1,2048]{2,1,0:T(1,128)}), f32[16,1,2048]{2,1,0:T(1,128)S(1)}, u32[]{:S(2)}, u32[]{:S(2)}) async-start(f32[16,1,2048]{2,1,0:T(1,128)} %broadcast_in_dim.59), calls=%async_computation.5 | async-start | bytes 262144 | tf_op jit(solution)/shard_map/all_to_all | solution.py:15
  348.5 8.7 %all-to-all-done.5 = f32[16,1,2048]{2,1,0:T(1,128)S(1)} async-done(((f32[16,1,2048]{2,1,0:T(1,128)}), f32[16,1,2048]{2,1,0:T(1,128)S(1)}, u32[]{:S(2)}, u32[]{:S(2)}) %all-to-all-start.5) | async-done | bytes 131104 | tf_op jit(solution)/shard_map/all_to_all | solution.py:15
  357.3 0.7 broadcast_in_dim.60
  358.0 4.8 %all-to-all-start.6 = ((f32[16,1,2048]{2,1,0:T(1,128)}), f32[16,1,2048]{2,1,0:T(1,128)S(1)}, u32[]{:S(2)}, u32[]{:S(2)}) async-start(f32[16,1,2048]{2,1,0:T(1,128)} %broadcast_in_dim.60), calls=%async_computation.6 | async-start | bytes 262144 | tf_op jit(solution)/shard_map/all_to_all | solution.py:15
  362.8 0.5 multiply_subtract_fusion
  363.4 6.3 %all-to-all-done.6 = f32[16,1,2048]{2,1,0:T(1,128)S(1)} async-done(((f32[16,1,2048]{2,1,0:T(1,128)}), f32[16,1,2048]{2,1,0:T(1,128)S(1)}, u32[]{:S(2)}, u32[]{:S(2)}) %all-to-all-start.6) | async-done | bytes 131104 | tf_op jit(solution)/shard_map/all_to_all | solution.py:15
  369.7 0.6 dynamic-slice_add_fusion
  (35 shorter events, 1.9 us)
Async XLA Ops:
  0.6 1.7 copy-start
  45.2 10.2 %copy-start.2 = (bf16[1024,72]{0,1:T(8,128)(2,1)S(1)}, bf16[1024,72]{0,1:T(8,128)(2,1)}, u32[]{:S(2)}) copy-start(bf16[1024,72]{0,1:T(8,128)(2,1)} %param.20) | copy-start | bytes 442372
  55.4 21.2 %copy-start.1 = (bf16[1024,72]{0,1:T(8,128)(2,1)S(1)}, bf16[1024,72]{0,1:T(8,128)(2,1)}, u32[]{:S(2)}) copy-start(bf16[1024,72]{0,1:T(8,128)(2,1)} %param.21) | copy-start | bytes 442372
  78.4 19.0 %all-to-all-start.3 = ((f32[64,1,1024]{2,1,0:T(1,128)}), f32[64,1,1024]{2,1,0:T(1,128)S(1)}, u32[]{:S(2)}, u32[]{:S(2)}) async-start(f32[64,1,1024]{2,1,0:T(1,128)} %broadcast_in_dim.57), calls=%async_computation.3 | async-start | bytes 524288 | tf_op jit(solution)/shard_map/all_to_all | solution.py:15
  103.6 6.4 %copy-start.5 = (s32[16]{0:T(128)S(1)}, s32[16]{0:T(128)}, u32[]{:S(2)}) copy-start(s32[16]{0:T(128)} %param.27) | copy-start | bytes 196
  103.6 6.4 %copy-start.6 = (f32[16]{0:T(128)S(1)}, f32[16]{0:T(128)}, u32[]{:S(2)}) copy-start(f32[16]{0:T(128)} %param.26) | copy-start | bytes 196
  103.6 221.0 %copy-start.4 = (s32[1024]{0:T(1024)S(1)}, s32[1024]{0:T(1024)}, u32[]{:S(2)}) copy-start(s32[1024]{0:T(1024)} %param.24) | copy-start | bytes 12292
  103.6 214.6 %all-to-all-start.4 = ((bf16[64,1024,72]{1,2,0:T(8,128)(2,1)}), bf16[64,1024,72]{1,2,0:T(8,128)(2,1)}, u32[]{:S(2)}, u32[]{:S(2)}) async-start(bf16[64,1024,72]{1,2,0:T(8,128)(2,1)} %stack.2), calls=%async_computation.4 | async-start | bytes 18874368 | tf_op jit(solution)/shard_map/all_to_all | solution.py:126
  318.8 21.6 %all-to-all-start.7 = ((f32[64,1,128]{2,1,0:T(1,128)}), f32[64,1,128]{2,1,0:T(1,128)S(1)}, u32[]{:S(2)}, u32[]{:S(2)}) async-start(f32[64,1,128]{2,1,0:T(1,128)} %broadcast_in_dim.100), calls=%async_computation.7 | async-start | bytes 65536 | tf_op jit(solution)/shard_map/all_to_all | solution.py:15
  324.6 45.1 %copy-start.3 = (f32[16]{0:T(128)S(1)}, f32[16]{0:T(128)}, u32[]{:S(2)}) copy-start(f32[16]{0:T(128)} %param.25) | copy-start | bytes 196
  341.1 16.1 %all-to-all-start.5 = ((f32[16,1,2048]{2,1,0:T(1,128)}), f32[16,1,2048]{2,1,0:T(1,128)S(1)}, u32[]{:S(2)}, u32[]{:S(2)}) async-start(f32[16,1,2048]{2,1,0:T(1,128)} %broadcast_in_dim.59), calls=%async_computation.5 | async-start | bytes 262144 | tf_op jit(solution)/shard_map/all_to_all | solution.py:15
  358.0 11.6 %all-to-all-start.6 = ((f32[16,1,2048]{2,1,0:T(1,128)}), f32[16,1,2048]{2,1,0:T(1,128)S(1)}, u32[]{:S(2)}, u32[]{:S(2)}) async-start(f32[16,1,2048]{2,1,0:T(1,128)} %broadcast_in_dim.60), calls=%async_computation.6 | async-start | bytes 262144 | tf_op jit(solution)/shard_map/all_to_all | solution.py:15
